TPU v7x, 512 devices: a whole 4x8x8 slice. The times are simulated.
512 devices in a mesh: row: 32 (over z_lo, y, core), col: 16 (over z_hi, x).
Axes of the slice: x: 4, y: 8, z: 8 (z_hi: 4, z_lo: 2; z = z_hi * 2 + z_lo), core: 2. Of those that a mesh axis runs over, the one named last changes fastest.
Arguments:
- pixels: float32 [8, 3, 1024, 2048], P(None, None, 'row', 'col'), may hold values from -6 to 6
- factor: float32 [1024, 512], P('row'), may hold values from -6 to 6
Outputs:
- gram: float32 [1024, 1024], P('row', 'col')
- projected: float32 [1024, 512], P('col', 'row')
All inputs are finite; a program needn't handle non-finite values.
Results may differ from a plain program's by a relative error of at most 0.000075.
Values sent between devices are 32-bit elements; how exact they have to be, the bound alone decides.
No kernel may reach another device: no remote copies, remote signals or barrier semaphores. Data moves between devices by JAX's collectives and lax.ppermute only.
A program may use at most 64 MiB of HBM per device.

v0:
```python
import jax
import jax.numpy as jnp
from jax import lax
from jax.sharding import PartitionSpec as P


def split_up(array, dim, size):
    before, after = (array.shape[:dim], array.shape[dim + 1 :])
    return jnp.moveaxis(array.reshape(*before, size, -1, *after), dim, 0)


def sum_at_owner(array, axis, dim):
    size = lax.axis_size(axis)
    parts = lax.all_to_all(split_up(array, dim, size), axis, 0, 0, tiled=True)
    return jnp.sum(parts, axis=0)


def pair_rows(own, others):
    return jnp.einsum(
        "vciw,vcjw->ij",
        own,
        others,
        precision=lax.Precision.HIGHEST,
        preferred_element_type=jnp.float32,
    )


def shards(pixels, factor):
    col_count = lax.axis_size("col")
    weight_scale = 1.0 / (pixels.shape[0] * pixels.shape[1] * pixels.shape[3] * col_count)
    partial_value = pair_rows(pixels, lax.all_gather(pixels, "row", axis=2, tiled=True))
    partial_value = partial_value * weight_scale
    block = sum_at_owner(partial_value, "col", 1)
    term = lax.dot_general(
        block,
        factor,
        (((0,), (0,)), ((), ())),
        precision=lax.Precision.HIGHEST,
        preferred_element_type=jnp.float32,
    )
    projected = sum_at_owner(term, "row", 1)
    return (block, projected)


def solution(mesh):
    in_specs = (P(None, None, "row", "col"), P("row", None))
    out_specs = (P("row", "col"), P("col", "row"))
    return jax.shard_map(shards, mesh=mesh, in_specs=in_specs, out_specs=out_specs, check_vma=False)
```

profile of v0, /device:TPU:1, one launch (start us, length us, event | category | flops | bytes accessed | tf_op | source)
XLA Modules:
  0.0 160.4 jit_solution(10644495970476327923)
XLA Ops:
  7.2 0.0 copy-start
  7.2 0.0 all-gather.2.cloned.1.call-start
  7.2 1.8 %copy.12 = f32[8,3,32,128]{3,2,0,1:T(8,128)} copy(f32[8,3,32,128]{3,2,1,0:T(8,128)} %param.2) | data formatting | bytes 786432 | tf_op args[0]
  9.0 0.0 all-gather.2.cloned.1.call-update
  9.0 89.4 %all-gather.2.cloned.1.call-done = f32[8,3,1024,128]{3,2,0,1:T(8,128)} async-done(((f32[8,3,32,128]{3,2,0,1:T(8,128)}), f32[8,3,1024,128]{3,2,0,1:T(8,128)}) %all-gather.2.cloned.1.call-update) | async-done | bytes 12582928 | tf_op jit(solution)/shard_map/all_gather | solution.py:31
  98.4 14.3 %fusion = f32[32,1024]{1,0:T(8,128)S(1)} fusion(f32[8,3,1024,128]{3,2,0,1:T(8,128)} %all-gather.2.cloned.1.call-done, f32[8,3,32,128]{3,2,1,0:T(8,128)} %param.2), kind=kOutput, calls=%fused_computation.2 | convolution fusion | flops 1207992320 | bytes 13107200 | tf_op jit(solution)/shard_map/vciw,vcjw->ij/dot_general | solution.py:19
  112.7 0.1 reshape.9
  112.8 0.1 copy.24
  112.9 0.8 reshape.12
  113.8 9.5 %all-to-all-start = ((f32[16,1,2048]{2,1,0:T(1,128)}), f32[16,1,2048]{2,1,0:T(1,128)S(1)}, u32[]{:S(2)}, u32[]{:S(2)}) async-start(f32[16,1,2048]{2,1,0:T(1,128)} %reshape.12), calls=%async_computation | async-start | bytes 262144 | tf_op jit(solution)/shard_map/all_to_all | solution.py:14
  123.3 0.0 copy-done
  123.3 0.1 copy.14
  123.4 9.2 %all-to-all-done = f32[16,1,2048]{2,1,0:T(1,128)S(1)} async-done(((f32[16,1,2048]{2,1,0:T(1,128)}), f32[16,1,2048]{2,1,0:T(1,128)S(1)}, u32[]{:S(2)}, u32[]{:S(2)}) %all-to-all-start) | async-done | bytes 131104 | tf_op jit(solution)/shard_map/all_to_all | solution.py:14
  132.6 0.5 broadcast
  133.1 0.9 reduce
  134.1 0.1 reshape.13
  134.2 0.0 copy-start.1
  134.2 0.4 convolution_bitcast_fusion
  134.6 0.2 copy.25
  134.8 0.2 reshape.14
  135.0 16.9 %all_to_all.10 = f32[32,1,1024]{2,1,0:T(1,128)S(1)} all-to-all(f32[32,1,1024]{2,1,0:T(1,128)S(1)} %reshape.14), channel_id=1, replica_groups=mesh['row'=32,'col'=16] {'row'}, dimensions={0} | all-to-all | bytes 262144 | tf_op jit(solution)/shard_map/all_to_all | solution.py:14
  151.9 1.0 reduce.1
  152.8 0.1 reshape.15
  152.9 0.6 bitcast_reduce_fusion
  153.6 0.0 copy-done.1
  (1 shorter events, 0.0 us)
Async XLA Ops:
  7.2 116.1 %copy-start = (f32[32,512]{1,0:T(8,128)S(1)}, f32[32,512]{1,0:T(8,128)}, u32[]{:S(2)}) copy-start(f32[32,512]{1,0:T(8,128)} %param.3) | copy-start | bytes 196612
  7.2 91.2 %all-gather.2.cloned.1.call-start = ((), (), s32[]{:S(2)}) async-start(), calls=%async_computation.2 | async-start | bytes 12976128 | tf_op jit(solution)/shard_map/all_gather | solution.py:31
  113.8 18.8 %all-to-all-start = ((f32[16,1,2048]{2,1,0:T(1,128)}), f32[16,1,2048]{2,1,0:T(1,128)S(1)}, u32[]{:S(2)}, u32[]{:S(2)}) async-start(f32[16,1,2048]{2,1,0:T(1,128)} %reshape.12), calls=%async_computation | async-start | bytes 262144 | tf_op jit(solution)/shard_map/all_to_all | solution.py:14
  134.2 19.4 %copy-start.1 = (f32[32,64]{1,0:T(8,128)}, f32[32,64]{1,0:T(8,128)S(1)}, u32[]{:S(2)}) copy-start(f32[32,64]{1,0:T(8,128)S(1)} %reduce_sum.18) | copy-start | bytes 24580
Sparse Core Ops, SparseCore 0:
  10.1 88.2 all-gather.1
where the time goes:
time: 161 us; the launch traced here: 160 us
  waiting for transfers between devices  98.6 us (61%)
  blocking collectives  16.9 us (10%)
  matrix products  14.7 us (9%)
  between operations  14.1 us (9%)
  starting transfers between devices  9.53 us (6%)
  local copies, waits for them, and re-layouts  3.99 us (2%)
  other arithmetic  2.57 us (2%)
    all_gather x1, waiting for transfers between devices, shards(): lax.all_gather(pixels, 'row', axis=2, tiled=True)  89.4 us
    all_to_all x1, blocking collectives, sum_at_owner(): parts = lax.all_to_all(split_up(array, dim, size), axis, 0, 0, tiled=True)  16.9 us
    dot_general x1, matrix products, pair_rows(): jnp.einsum('vciw,vcjw->ij', own, others, precision=lax.Precision.HIGHEST,...  14.3 us
    all_to_all x1, starting transfers between devices, sum_at_owner(): parts = lax.all_to_all(split_up(array, dim, size), axis, 0, 0, tiled=True)  9.49 us
    all_to_all x1, waiting for transfers between devices, sum_at_owner(): parts = lax.all_to_all(split_up(array, dim, size), axis, 0, 0, tiled=True)  9.19 us
  transfers between devices with their start and end apart: 2, of which 2 were waited for; matrix products, arithmetic and copies ran while one was open for 0% of the time, Pallas kernels for 0%

commit v1 on v0

--- a/solution.py
+++ b/solution.py
@@ -28,7 +28,12 @@
 def shards(pixels, factor):
     col_count = lax.axis_size("col")
     weight_scale = 1.0 / (pixels.shape[0] * pixels.shape[1] * pixels.shape[3] * col_count)
-    partial_value = pair_rows(pixels, lax.all_gather(pixels, "row", axis=2, tiled=True))
+    partial_value = pair_rows(
+        pixels,
+        jnp.concatenate(
+            lax.all_to_all(jnp.stack([pixels] * lax.axis_size("row")), "row", 0, 0), axis=2
+        ),
+    )
     partial_value = partial_value * weight_scale
     block = sum_at_owner(partial_value, "col", 1)
     term = lax.dot_general(

time: 161 us -> 356 us (2.21)
  blocking collectives: 16.9 us -> 300 us
  waiting for transfers between devices: 98.6 us -> 9.22 us
  between operations: 14.1 us -> 0.74 us
  local copies, waits for them, and re-layouts: 3.99 us -> 16.2 us
    all_to_all x0 -> x1, blocking collectives: none -> 284 us  [shards(): lax.all_to_all(jnp.stack([pixels] * lax.axis_size('row')), 'row', 0, 0)]
    all_gather x1 -> x0, waiting for transfers between devices: 89.4 us -> none  [shards(): lax.all_gather(pixels, 'row', axis=2, tiled=True)]
    reshape x0 -> x1, local copies, waits for them, and re-layouts: none -> 11.4 us  [shards(): jnp.concatenate(lax.all_to_all(jnp.stack([pixels] * lax.axis_size('row'))...]
  transfers between devices with their start and end apart: 2 -> 1, of which waited for: 2 -> 1; matrix products, arithmetic and copies ran while one was open for 0% -> 0% of each run, Pallas kernels for 0% -> 0%
where the time goes in v1:
time: 356 us; the launch traced here: 355 us
  blocking collectives  300 us (84%)
  local copies, waits for them, and re-layouts  16.2 us (5%)
  matrix products  14.7 us (4%)
  starting transfers between devices  11.7 us (3%)
  waiting for transfers between devices  9.22 us (3%)
    all_to_all x1, blocking collectives, shards(): lax.all_to_all(jnp.stack([pixels] * lax.axis_size('row')), 'row', 0, 0)  284 us
    all_to_all x1, blocking collectives, sum_at_owner(): parts = lax.all_to_all(split_up(array, dim, size), axis, 0, 0, tiled=True)  16.1 us
    dot_general x1, matrix products, pair_rows(): jnp.einsum('vciw,vcjw->ij', own, others, precision=lax.Precision.HIGHEST,...  14.3 us
    all_to_all x1, starting transfers between devices, sum_at_owner(): parts = lax.all_to_all(split_up(array, dim, size), axis, 0, 0, tiled=True)  11.7 us
    reshape x1, local copies, waits for them, and re-layouts, shards(): jnp.concatenate(lax.all_to_all(jnp.stack([pixels] * lax.axis_size('row'))...  11.4 us
    all_to_all x1, waiting for transfers between devices, sum_at_owner(): parts = lax.all_to_all(split_up(array, dim, size), axis, 0, 0, tiled=True)  9.22 us
  transfers between devices with their start and end apart: 1, of which 1 were waited for; matrix products, arithmetic and copies ran while one was open for 0% of the time, Pallas kernels for 0%

profile of v1, /device:TPU:1, one launch (start us, length us, event | category | flops | bytes accessed | tf_op | source)
XLA Modules:
  0.0 355.4 jit_solution(3980428004158320097)
XLA Ops:
  0.6 1.0 copy.13
  1.7 1.6 stack.2
  3.3 284.2 %all_to_all.15 = f32[32,8,3,32,128]{4,3,1,2,0:T(8,128)} all-to-all(f32[32,8,3,32,128]{4,3,1,2,0:T(8,128)S(1)} %stack.2), channel_id=1, replica_groups=mesh['row'=32,'col'=16] {'row'}, dimensions={0} | all-to-all | bytes 25165824 | tf_op jit(solution)/shard_map/all_to_all | solution.py:34
  287.4 0.0 copy-start
  287.4 11.4 %copy.12 = f32[8,3,32,32,128]{4,3,2,0,1:T(8,128)} copy(f32[8,3,32,32,128]{4,3,0,1,2:T(8,128)} %bitcast.25) | data formatting | bytes 25165824 | tf_op jit(solution)/shard_map/reshape | solution.py:33
  298.8 0.0 copy-start.1
  298.8 0.0 copy-done
  298.8 14.3 %fusion = f32[32,1024]{1,0:T(8,128)S(1)} fusion(f32[8,3,1024,128]{3,2,0,1:T(8,128)} %bitcast.26, f32[8,3,32,128]{3,2,1,0:T(8,128)S(1)} %copy-done), kind=kOutput, calls=%fused_computation.2 | convolution fusion | flops 1207992320 | bytes 13107200 | tf_op jit(solution)/shard_map/vciw,vcjw->ij/dot_general | solution.py:19
  313.2 0.1 reshape.19
  313.3 0.1 copy.25
  313.4 0.8 reshape.22
  314.2 11.7 %all-to-all-start.1 = ((f32[16,1,2048]{2,1,0:T(1,128)}), f32[16,1,2048]{2,1,0:T(1,128)S(1)}, u32[]{:S(2)}, u32[]{:S(2)}) async-start(f32[16,1,2048]{2,1,0:T(1,128)} %reshape.22), calls=%async_computation.1 | async-start | bytes 262144 | tf_op jit(solution)/shard_map/all_to_all | solution.py:14
  325.9 0.0 copy-done.1
  325.9 0.1 copy.15
  326.0 9.2 %all-to-all-done.1 = f32[16,1,2048]{2,1,0:T(1,128)S(1)} async-done(((f32[16,1,2048]{2,1,0:T(1,128)}), f32[16,1,2048]{2,1,0:T(1,128)S(1)}, u32[]{:S(2)}, u32[]{:S(2)}) %all-to-all-start.1) | async-done | bytes 131104 | tf_op jit(solution)/shard_map/all_to_all | solution.py:14
  335.2 0.5 broadcast.2
  335.7 0.9 reduce
  336.7 0.1 reshape.23
  336.8 0.0 copy-start.2
  336.9 0.4 convolution_bitcast_fusion
  337.2 0.2 copy.26
  337.4 0.2 reshape.24
  337.6 16.1 %all_to_all.16 = f32[32,1,1024]{2,1,0:T(1,128)S(1)} all-to-all(f32[32,1,1024]{2,1,0:T(1,128)S(1)} %reshape.24), channel_id=1, replica_groups=mesh['row'=32,'col'=16] {'row'}, dimensions={0} | all-to-all | bytes 262144 | tf_op jit(solution)/shard_map/all_to_all | solution.py:14
  353.7 1.0 reduce.1
  354.7 0.1 reshape.25
  354.8 0.6 bitcast_reduce_fusion
  355.4 0.0 copy-done.2
  (1 shorter events, 0.0 us)
Async XLA Ops:
  287.4 11.4 %copy-start = (f32[8,3,32,128]{3,2,1,0:T(8,128)S(1)}, f32[8,3,32,128]{3,2,1,0:T(8,128)}, u32[]{:S(2)}) copy-start(f32[8,3,32,128]{3,2,1,0:T(8,128)} %param.2) | copy-start | bytes 1179652
  298.8 27.1 %copy-start.1 = (f32[32,512]{1,0:T(8,128)S(1)}, f32[32,512]{1,0:T(8,128)}, u32[]{:S(2)}) copy-start(f32[32,512]{1,0:T(8,128)} %param.3) | copy-start | bytes 196612
  314.2 21.1 %all-to-all-start.1 = ((f32[16,1,2048]{2,1,0:T(1,128)}), f32[16,1,2048]{2,1,0:T(1,128)S(1)}, u32[]{:S(2)}, u32[]{:S(2)}) async-start(f32[16,1,2048]{2,1,0:T(1,128)} %reshape.22), calls=%async_computation.1 | async-start | bytes 262144 | tf_op jit(solution)/shard_map/all_to_all | solution.py:14
  336.8 18.6 %copy-start.2 = (f32[32,64]{1,0:T(8,128)}, f32[32,64]{1,0:T(8,128)S(1)}, u32[]{:S(2)}) copy-start(f32[32,64]{1,0:T(8,128)S(1)} %reduce_sum.18) | copy-start | bytes 24580
